TPU v7x, 128 devices: a whole 4x4x4 slice. The times are simulated.
128 devices in a mesh: expert: 16 (over y, x_hi, core), replica: 8 (over z, x_lo).
Axes of the slice: x: 4 (x_hi: 2, x_lo: 2; x = x_hi * 2 + x_lo), y: 4, z: 4, core: 2. Of those that a mesh axis runs over, the one named last changes fastest.
Arguments:
- tokens_in: bfloat16 [32768, 2048], P(('expert', 'replica')), may hold values from -6 to 6
- cotangents: bfloat16 [32768, 8192], P(('expert', 'replica')), may hold values from -0.1796875 to 0.1796875
- left_root: bfloat16 [16, 2048, 2048], P('expert'), may hold values from -2 to 6, as said below
- right_root: bfloat16 [16, 8, 1024, 1024], P('expert', 'replica'), may hold values from -2 to 6, as said below
Outputs:
- update: bfloat16 [16, 2048, 8192], P('expert', None, 'replica')
Inputs may be any that keep to these rules, and one draw needn't show every extreme that they name: `left_root`: each matrix is symmetric. `right_root`: each block is symmetric.
All inputs are finite; a program needn't handle non-finite values.
Results may differ from a plain program's by a relative error of at most 0.0058.
Values may be sent and summed in bfloat16 or wider, within the bound.
No kernel may reach another device: no remote copies, remote signals or barrier semaphores. Data moves between devices by JAX's collectives and lax.ppermute only.
A program may use at most 192 MiB of HBM per device.

v0:
```python
import jax
import jax.numpy as jnp
from jax import lax
from jax.experimental import pallas as pl
from jax.experimental.pallas import tpu as pltpu
from jax.sharding import Mesh
from jax.sharding import PartitionSpec as P

EXPERT = ("y", "xh", "c")
REPLICA = ("z", "xl")
PLANE = ("xl", "y", "xh", "c")
BF16 = jnp.bfloat16
F32 = jnp.float32


def shift(value, axis, step):
    size = lax.axis_size(axis)
    return lax.ppermute(value, axis, [(i, (i + step) % size) for i in range(size)])


def exchange(value, axes):
    return lax.all_to_all(value, axes, split_axis=0, concat_axis=0, tiled=True)


def packed(cotangents, steps, groups, width):
    rows = cotangents.shape[0]
    z_size = lax.axis_size("z")

    def kernel(source, *refs):
        targets, semaphore = refs[:-1], refs[-1]
        z = lax.axis_index("z")
        copies = []
        for target, step in zip(targets, steps):
            first = ((z + step) % z_size) * (groups * width)
            for g in range(groups):
                copies.append(
                    pltpu.make_async_copy(
                        source.at[:, pl.ds(pl.multiple_of(first + g * width, width), width)],
                        target.at[g],
                        semaphore.at[len(copies)],
                    )
                )
        for copy in copies:
            copy.start()
        for copy in copies:
            copy.wait()

    return pl.pallas_call(
        kernel,
        in_specs=[pl.BlockSpec(memory_space=pl.ANY)],
        out_specs=[pl.BlockSpec(memory_space=pl.ANY)] * len(steps),
        out_shape=[jax.ShapeDtypeStruct((groups, rows, width), cotangents.dtype)] * len(steps),
        scratch_shapes=[pltpu.SemaphoreType.DMA((len(steps) * groups,))],
        name="packed",
    )(cotangents)


def left_applied(left, tokens):
    order, count = left.shape[0], tokens.shape[0]
    half = order // 2

    def kernel(left_ref, tokens_ref, low_ref, high_ref):
        value = lax.dot_general(
            left_ref[...], tokens_ref[...], (((1,), (1,)), ((), ())), preferred_element_type=F32
        ).astype(BF16)

        @pl.when(pl.program_id(0) == 0)
        def _():
            low_ref[...] = value

        @pl.when(pl.program_id(0) == 1)
        def _():
            high_ref[...] = value

    return pl.pallas_call(
        kernel,
        grid=(2,),
        in_specs=[
            pl.BlockSpec((half, order), lambda i: (i, 0)),
            pl.BlockSpec((count, order), lambda i: (0, 0)),
        ],
        out_specs=[pl.BlockSpec((half, count), lambda i: (0, 0))] * 2,
        out_shape=[jax.ShapeDtypeStruct((half, count), BF16)] * 2,
        compiler_params=pltpu.CompilerParams(dimension_semantics=("arbitrary",)),
        name="left_applied",
    )(left, tokens)


def combined(side, lows, highs, rights, base, out_type):
    half, count = lows[0].shape
    width = rights[0][0].shape[-1]
    tile = 256
    steps = half // tile
    pieces = len(lows)

    def kernel(side_ref, *refs):
        low_refs, high_refs = refs[:pieces], refs[pieces : 2 * pieces]
        right_refs = refs[2 * pieces : 3 * pieces]
        out_ref = refs[-1]
        is_low = pl.program_id(0) < steps

        def run(left_refs):
            left = jnp.concatenate([r[...] for r in left_refs], axis=1)
            right = jnp.concatenate([r[...].reshape(count, width) for r in right_refs], axis=0)
            total = jnp.dot(left, right, preferred_element_type=F32)
            if base is not None:
                total = total + refs[3 * pieces][...]
            out_ref[...] = total.astype(out_type)

        @pl.when(is_low)
        def _():
            run(low_refs)

        @pl.when(jnp.logical_not(is_low))
        def _():
            run(high_refs)

    low_spec = pl.BlockSpec((tile, count), lambda i, side: (jnp.minimum(i, steps - 1), 0))
    high_spec = pl.BlockSpec((tile, count), lambda i, side: (jnp.maximum(i - steps, 0), 0))
    row_spec = pl.BlockSpec((tile, width), lambda i, side: (i, 0))
    right_specs = []
    for value, other, k in rights:
        if k is None:
            right_specs.append(pl.BlockSpec((1, count, width), lambda i, side, o=other: ((side[0] + o) % 2, 0, 0)))
        else:
            block = (1, value.shape[1], 1, value.shape[3], width)
            right_specs.append(pl.BlockSpec(block, lambda i, side, o=other, k=k: ((side[0] + o) % 2, 0, k, 0, 0)))
    bases = [] if base is None else [base]
    return pl.pallas_call(
        kernel,
        grid_spec=pltpu.PrefetchScalarGridSpec(
            num_scalar_prefetch=1,
            grid=(2 * steps,),
            in_specs=[low_spec] * pieces + [high_spec] * pieces + right_specs + [row_spec] * len(bases),
            out_specs=row_spec,
        ),
        out_shape=jax.ShapeDtypeStruct((2 * half, width), out_type),
        compiler_params=pltpu.CompilerParams(dimension_semantics=("arbitrary",)),
        name="combined",
    )(side.reshape(1), *lows, *highs, *[r[0] for r in rights], *bases)


def body(tokens_in, cotangents, left_root, right_root):
    left, right = left_root[0], right_root[0, 0]
    width = right.shape[0]
    order = left.shape[0]
    experts = lax.axis_size(EXPERT)
    plane = lax.axis_size(PLANE)
    slots = tokens_in.shape[0] // experts
    z_size = lax.axis_size("z")
    side, sides = lax.axis_index("xl"), lax.axis_size("xl")

    sent = packed(cotangents, (2, 1, 3), sides, width)
    sent = [v.reshape(plane, slots, width) for v in sent]
    far, up, down = shift(sent[0], "z", 2), shift(sent[1], "z", 1), shift(sent[2], "z", -1)
    kept = packed(cotangents, (0,), sides, width)[0].reshape(plane, slots, width)

    tokens = exchange(tokens_in.reshape(experts, slots, order), EXPERT)
    low, high = left_applied(left, tokens.reshape(experts * slots, order))
    low_other, high_other = shift(low, "xl", 1), shift(high, "xl", 1)

    own = exchange(kept, PLANE)
    rest = exchange(jnp.stack([up, down, far], axis=1), PLANE)

    lows, highs = [], []
    for a, b in ((low, high), (low_other, high_other)):
        a_up, b_down = shift(a, "z", 1), shift(b, "z", -1)
        a_down, b_up = shift(a, "z", -1), shift(b, "z", 1)
        a_far, b_far = shift(a_up, "z", 1), shift(b_down, "z", -1)
        lows.append((a, a_up, a_down, a_far))
        highs.append((b, b_up, b_down, b_far))

    own = jnp.dot(own.reshape(-1, width), right, preferred_element_type=F32).astype(BF16)
    rest = jnp.dot(rest.reshape(-1, width), right, preferred_element_type=F32).astype(BF16)
    own = own.reshape(sides, experts * slots, width)
    rest = rest.reshape(sides, experts, z_size - 1, slots, width)
    most = combined(
        side,
        [v for row in lows for v in row[:3]],
        [v for row in highs for v in row[:3]],
        [r for o in (0, 1) for r in ((own, o, None), (rest, o, 0), (rest, o, 1))],
        None,
        F32,
    )
    update = combined(
        side, [row[3] for row in lows], [row[3] for row in highs], [(rest, 0, 2), (rest, 1, 2)], most, BF16
    )
    return update[None]


def solution(mesh):
    split = Mesh(mesh.devices.reshape(4, 2, 2, 4, 2), EXPERT + REPLICA)
    rows = P(EXPERT + REPLICA, None)
    placed = (rows, rows, P(EXPERT, None, None), P(EXPERT, REPLICA, None, None))

    return jax.shard_map(body, mesh=split, in_specs=placed, out_specs=P(EXPERT, None, REPLICA), check_vma=False)
```

profile of v0, /device:TPU:22, one launch (start us, length us, event | category | flops | bytes accessed | tf_op | source)
XLA Modules:
  0.0 296.0 jit_solution(13174214077729629237)
XLA Ops:
  0.0 7.4 %all-to-all-start = ((bf16[16,16,2048]{2,1,0:T(8,128)(2,1)}), bf16[16,16,2048]{2,1,0:T(8,128)(2,1)S(1)}, u32[]{:S(2)}, u32[]{:S(2)}) async-start(bf16[16,16,2048]{2,1,0:T(8,128)(2,1)} %bitcast.36), calls=%async_computation | async-start | bytes 2097152 | tf_op jit(solution)/shard_map/all_to_all | solution.py:22
  7.4 96.4 %packed.2 = (bf16[2,256,1024]{2,1,0:T(8,128)(2,1)}, bf16[2,256,1024]{2,1,0:T(8,128)(2,1)}, bf16[2,256,1024]{2,1,0:T(8,128)(2,1)}) custom-call(bf16[256,8192]{1,0:T(8,128)(2,1)} %source.3), custom_call_target="tpu_custom_call" | custom-call | tf_op jit(solution)/shard_map/packed/pallas_call | solution.py:48
  103.8 2.0 collective-permute-start.10
  105.8 2.2 collective-permute-start.11
  108.0 1.8 collective-permute-start.12
  109.8 32.9 %packed.3 = bf16[2,256,1024]{2,1,0:T(8,128)(2,1)} custom-call(bf16[256,8192]{1,0:T(8,128)(2,1)} %source.3), custom_call_target="tpu_custom_call" | custom-call | tf_op jit(solution)/shard_map/packed/pallas_call | solution.py:48
  142.7 0.0 all-to-all-done
  142.7 7.5 %all-to-all-start.2 = ((bf16[32,16,1024]{2,1,0:T(8,128)(2,1)}), bf16[32,16,1024]{2,1,0:T(8,128)(2,1)}, u32[]{:S(2)}, u32[]{:S(2)}) async-start(bf16[32,16,1024]{2,1,0:T(8,128)(2,1)} %bitcast.35), calls=%async_computation.2 | async-start | bytes 2097152 | tf_op jit(solution)/shard_map/all_to_all | solution.py:22
  150.2 0.0 collective-permute-done.10
  150.2 3.3 %collective-permute-done.11 = bf16[32,16,1024]{2,1,0:T(8,128)(2,1)} collective-permute-done((bf16[32,16,1024]{2,1,0:T(8,128)(2,1)}, bf16[32,16,1024]{2,1,0:T(8,128)(2,1)}, u32[]{:S(2)}, u32[]{:S(2)}) %collective-permute-start.11) | collective-permute-done | bytes 1048608 | tf_op jit(solution)/shard_map/ppermute | solution.py:18
  153.5 1.8 collective-permute-done.12
  155.3 3.8 %pad_maximum_fusion = bf16[32,3,16,1024]{3,2,1,0:T(8,128)(2,1)} fusion(bf16[32,1,16,1024]{3,2,1,0:T(8,128)(2,1)} %bitcast.9, bf16[32,1,16,1024]{3,2,1,0:T(8,128)(2,1)} %bitcast.7, bf16[32,1,16,1024]{3,2,1,0:T(8,128)(2,1)} %bitcast.5), kind=kLoop, calls=%fused_computation.1 | loop fusion | flops 3145728 | bytes 6291456 | tf_op jit(solution)/shard_map/stack | solution.py:163
  159.2 4.5 %all-to-all-done.2 = bf16[32,16,1024]{2,1,0:T(8,128)(2,1)} async-done(((bf16[32,16,1024]{2,1,0:T(8,128)(2,1)}), bf16[32,16,1024]{2,1,0:T(8,128)(2,1)}, u32[]{:S(2)}, u32[]{:S(2)}) %all-to-all-start.2) | async-done | bytes 1048608 | tf_op jit(solution)/shard_map/all_to_all | solution.py:22
  163.7 8.0 %all-to-all-start.1 = ((bf16[32,3,16,1024]{3,2,1,0:T(8,128)(2,1)}), bf16[32,3,16,1024]{3,2,1,0:T(8,128)(2,1)}, u32[]{:S(2)}, u32[]{:S(2)}) async-start(bf16[32,3,16,1024]{3,2,1,0:T(8,128)(2,1)} %pad_maximum_fusion), calls=%async_computation.1 | async-start | bytes 6291456 | tf_op jit(solution)/shard_map/all_to_all | solution.py:22
  171.7 6.2 %left_applied.1 = (bf16[1024,256]{1,0:T(8,128)(2,1)}, bf16[1024,256]{1,0:T(8,128)(2,1)}) custom-call(bf16[2048,2048]{1,0:T(8,128)(2,1)} %bitcast.31, bf16[256,2048]{1,0:T(8,128)(2,1)} %bitcast.34), custom_call_target="tpu_custom_call" | custom-call | tf_op jit(solution)/shard_map/left_applied/pallas_call | solution.py:75
  177.9 0.7 collective-permute-start.2
  178.6 1.3 collective-permute-start.7
  179.9 1.0 collective-permute-start
  180.9 2.2 collective-permute-start.5
  183.1 0.0 collective-permute-start.13
  183.1 40.5 %collective-permute-done.2.refs_3_ = bf16[1024,256]{1,0:T(8,128)(2,1)S(1)} collective-permute-done((bf16[1024,256]{1,0:T(8,128)(2,1)}, bf16[1024,256]{1,0:T(8,128)(2,1)S(1)}, u32[]{:S(2)}, u32[]{:S(2)}) %collective-permute-start.2) | collective-permute-done | bytes 524320 | tf_op jit(solution)/shard_map/ppermute | solution.py:18
  223.6 1.0 collective-permute-start.15
  224.7 9.7 %collective-permute-done.7.refs_9_ = bf16[1024,256]{1,0:T(8,128)(2,1)} collective-permute-done((bf16[1024,256]{1,0:T(8,128)(2,1)}, bf16[1024,256]{1,0:T(8,128)(2,1)}, u32[]{:S(2)}, u32[]{:S(2)}) %collective-permute-start.7) | collective-permute-done | bytes 524320 | tf_op jit(solution)/shard_map/ppermute | solution.py:18
  234.4 1.0 collective-permute-start.3
  235.4 0.0 collective-permute-done.refs_1_
  235.4 2.2 collective-permute-start.8
  237.7 0.0 collective-permute-done.5.refs_8_
  237.7 0.1 collective-permute-start.14
  237.7 3.5 %fusion.3 = bf16[512,1024]{1,0:T(8,128)(2,1)} fusion(bf16[512,1024]{1,0:T(8,128)(2,1)} %bitcast.14, bf16[1,1,1024,1024]{3,2,1,0:T(8,128)(2,1)S(1)} %copy-done), kind=kOutput, calls=%fused_computation.5 | convolution fusion | flops 1074266112 | bytes 4194304 | tf_op jit(solution)/shard_map/dot_general | solution.py:173
  241.2 0.0 collective-permute-done.13.refs_2_
  241.2 1.9 collective-permute-start.16
  243.2 0.0 collective-permute-done.15.refs_7_
  243.2 0.1 collective-permute-start.1
  243.3 7.3 %collective-permute-done.3.refs_4_ = bf16[1024,256]{1,0:T(8,128)(2,1)} collective-permute-done((bf16[1024,256]{1,0:T(8,128)(2,1)S(1)}, bf16[1024,256]{1,0:T(8,128)(2,1)}, u32[]{:S(2)}, u32[]{:S(2)}) %collective-permute-start.3) | collective-permute-done | bytes 524320 | tf_op jit(solution)/shard_map/ppermute | solution.py:18
  250.5 0.0 collective-permute-start.6
  250.5 0.0 collective-permute-done.8.refs_11_
  250.5 2.0 collective-permute-start.4
  252.6 9.2 %collective-permute-done.14.refs_5_ = bf16[1024,256]{1,0:T(8,128)(2,1)} collective-permute-done((bf16[1024,256]{1,0:T(8,128)(2,1)S(1)}, bf16[1024,256]{1,0:T(8,128)(2,1)}, u32[]{:S(2)}, u32[]{:S(2)}) %collective-permute-start.14) | collective-permute-done | bytes 524320 | tf_op jit(solution)/shard_map/ppermute | solution.py:18
  261.8 3.4 %collective-permute-start.9 = (bf16[1024,256]{1,0:T(8,128)(2,1)}, bf16[1024,256]{1,0:T(8,128)(2,1)S(1)}, u32[]{:S(2)}, u32[]{:S(2)}) collective-permute-start(bf16[1024,256]{1,0:T(8,128)(2,1)} %collective-permute-done.8.refs_11_), channel_id=1, source_target_pairs={{0,6},{2,0},{4,2},{6,4},{1,7},{3,1},{5,3},{7,5},{8,14},{10,8},{12,... | collective-permute-start | bytes 1572872 | tf_op jit(solution)/shard_map/ppermute | solution.py:18
  265.2 0.0 all-to-all-done.1
  265.2 6.7 %convolution_convert_fusion = bf16[1536,1024]{1,0:T(8,128)(2,1)} fusion(bf16[1536,1024]{1,0:T(8,128)(2,1)} %bitcast.10, bf16[1,1,1024,1024]{3,2,1,0:T(8,128)(2,1)S(1)} %copy-done), kind=kOutput, calls=%fused_computation | convolution fusion | flops 3222798336 | bytes 8388608 | tf_op jit(solution)/shard_map/dot_general | solution.py:174
  271.9 0.0 collective-permute-done.16.refs_10_
  271.9 13.4 %combined.2.refs_6_ = f32[2048,1024]{1,0:T(8,128)} custom-call(s32[1]{0:T(128)} %bitcast.side_ref, bf16[1024,256]{1,0:T(8,128)(2,1)} %get-tuple-element.10.refs_0_, bf16[1024,256]{1,0:T(8,128)(2,1)} %copy-done.3, bf16[1024,256]{1,0:T(8,128)(2,1)} %collective-permute-done.13.refs_2_, bf16[1024,256]{1,0:T(8,128)(2,1)} %copy-done.2, ...), custom_call_target="tpu_custom_call" | custom-call | tf_op jit(solution)/shard_map/combined/pallas_call | solution.py:129
  285.3 0.0 collective-permute-done.1.refs_0_
  285.3 0.0 collective-permute-done.6.refs_2_
  285.3 0.0 collective-permute-done.4.refs_1_
  285.4 0.8 copy-done.4
  286.2 9.9 %combined.3 = bf16[2048,1024]{1,0:T(8,128)(2,1)} custom-call(s32[1]{0:T(128)} %bitcast.side_ref, bf16[1024,256]{1,0:T(8,128)(2,1)} %collective-permute-done.1.refs_0_, bf16[1024,256]{1,0:T(8,128)(2,1)} %collective-permute-done.4.refs_1_, bf16[1024,256]{1,0:T(8,128)(2,1)} %collective-permute-done.6.refs_2_, bf16[1024,256]{1,0:T(8,128)(2,1)} %copy-done.4, ...), custom_call_target="tpu_custom_call" | custom-call | tf_op jit(solution)/shard_map/combined/pallas_call | solution.py:129
  (10 shorter events, 0.0 us)
Async XLA Ops:
  0.0 237.7 %copy-start = (bf16[1,1,1024,1024]{3,2,1,0:T(8,128)(2,1)S(1)}, bf16[1,1,1024,1024]{3,2,1,0:T(8,128)(2,1)}, u32[]{:S(2)}) copy-start(bf16[1,1,1024,1024]{3,2,1,0:T(8,128)(2,1)} %param.7) | copy-start | bytes 6291460
  0.0 142.7 %all-to-all-start = ((bf16[16,16,2048]{2,1,0:T(8,128)(2,1)}), bf16[16,16,2048]{2,1,0:T(8,128)(2,1)S(1)}, u32[]{:S(2)}, u32[]{:S(2)}) async-start(bf16[16,16,2048]{2,1,0:T(8,128)(2,1)} %bitcast.36), calls=%async_computation | async-start | bytes 2097152 | tf_op jit(solution)/shard_map/all_to_all | solution.py:22
  103.8 46.4 %collective-permute-start.10 = (bf16[32,16,1024]{2,1,0:T(8,128)(2,1)}, bf16[32,16,1024]{2,1,0:T(8,128)(2,1)}, u32[]{:S(2)}, u32[]{:S(2)}) collective-permute-start(bf16[32,16,1024]{2,1,0:T(8,128)(2,1)} %bitcast.39), channel_id=1, source_target_pairs={{0,2},{2,4},{4,6},{6,0},{1,3},{3,5},{5,7},{7,1},{8,10},{10,12},{12... | collective-permute-start | bytes 3145736 | tf_op jit(solution)/shard_map/ppermute | solution.py:18
  105.8 47.7 %collective-permute-start.11 = (bf16[32,16,1024]{2,1,0:T(8,128)(2,1)}, bf16[32,16,1024]{2,1,0:T(8,128)(2,1)}, u32[]{:S(2)}, u32[]{:S(2)}) collective-permute-start(bf16[32,16,1024]{2,1,0:T(8,128)(2,1)} %bitcast.38), channel_id=1, source_target_pairs={{0,6},{2,0},{4,2},{6,4},{1,7},{3,1},{5,3},{7,5},{8,14},{10,8},{12,... | collective-permute-start | bytes 3145736 | tf_op jit(solution)/shard_map/ppermute | solution.py:18
  108.0 47.3 %collective-permute-start.12 = (bf16[32,16,1024]{2,1,0:T(8,128)(2,1)}, bf16[32,16,1024]{2,1,0:T(8,128)(2,1)}, u32[]{:S(2)}, u32[]{:S(2)}) collective-permute-start(bf16[32,16,1024]{2,1,0:T(8,128)(2,1)} %bitcast.37), channel_id=1, source_target_pairs={{0,4},{2,6},{4,0},{6,2},{1,5},{3,7},{5,1},{7,3},{8,12},{10,14},{12... | collective-permute-start | bytes 3145736 | tf_op jit(solution)/shard_map/ppermute | solution.py:18
  142.7 16.5 %copy-start.1 = (bf16[16,16,2048]{2,1,0:T(8,128)(2,1)}, bf16[16,16,2048]{2,1,0:T(8,128)(2,1)S(1)}, u32[]{:S(2)}) copy-start(bf16[16,16,2048]{2,1,0:T(8,128)(2,1)S(1)} %all-to-all-done) | copy-start | bytes 3145732
  142.7 21.0 %all-to-all-start.2 = ((bf16[32,16,1024]{2,1,0:T(8,128)(2,1)}), bf16[32,16,1024]{2,1,0:T(8,128)(2,1)}, u32[]{:S(2)}, u32[]{:S(2)}) async-start(bf16[32,16,1024]{2,1,0:T(8,128)(2,1)} %bitcast.35), calls=%async_computation.2 | async-start | bytes 2097152 | tf_op jit(solution)/shard_map/all_to_all | solution.py:22
  163.7 101.5 %all-to-all-start.1 = ((bf16[32,3,16,1024]{3,2,1,0:T(8,128)(2,1)}), bf16[32,3,16,1024]{3,2,1,0:T(8,128)(2,1)}, u32[]{:S(2)}, u32[]{:S(2)}) async-start(bf16[32,3,16,1024]{3,2,1,0:T(8,128)(2,1)} %pad_maximum_fusion), calls=%async_computation.1 | async-start | bytes 6291456 | tf_op jit(solution)/shard_map/all_to_all | solution.py:22
  177.9 45.8 %collective-permute-start.2 = (bf16[1024,256]{1,0:T(8,128)(2,1)}, bf16[1024,256]{1,0:T(8,128)(2,1)S(1)}, u32[]{:S(2)}, u32[]{:S(2)}) collective-permute-start(bf16[1024,256]{1,0:T(8,128)(2,1)} %get-tuple-element.10.refs_0_), channel_id=1, source_target_pairs={{0,1},{1,0},{2,3},{3,2},{4,5},{5,4},{6,7},{7,6},{8,9},{9,8},{10,11... | collective-permute-start | bytes 1572872 | tf_op jit(solution)/shard_map/ppermute | solution.py:18
  178.6 55.8 %collective-permute-start.7 = (bf16[1024,256]{1,0:T(8,128)(2,1)}, bf16[1024,256]{1,0:T(8,128)(2,1)}, u32[]{:S(2)}, u32[]{:S(2)}) collective-permute-start(bf16[1024,256]{1,0:T(8,128)(2,1)} %get-tuple-element.11.refs_6_), channel_id=1, source_target_pairs={{0,1},{1,0},{2,3},{3,2},{4,5},{5,4},{6,7},{7,6},{8,9},{9,8},{10,11... | collective-permute-start | bytes 1572872 | tf_op jit(solution)/shard_map/ppermute | solution.py:18
  179.9 55.5 %collective-permute-start = (bf16[1024,256]{1,0:T(8,128)(2,1)}, bf16[1024,256]{1,0:T(8,128)(2,1)S(1)}, u32[]{:S(2)}, u32[]{:S(2)}) collective-permute-start(bf16[1024,256]{1,0:T(8,128)(2,1)} %get-tuple-element.10.refs_0_), channel_id=1, source_target_pairs={{0,2},{2,4},{4,6},{6,0},{1,3},{3,5},{5,7},{7,1},{8,10},{10,12},{12... | collective-permute-start | bytes 1572872 | tf_op jit(solution)/shard_map/ppermute | solution.py:18
  180.9 56.8 %collective-permute-start.5 = (bf16[1024,256]{1,0:T(8,128)(2,1)}, bf16[1024,256]{1,0:T(8,128)(2,1)}, u32[]{:S(2)}, u32[]{:S(2)}) collective-permute-start(bf16[1024,256]{1,0:T(8,128)(2,1)} %get-tuple-element.11.refs_6_), channel_id=1, source_target_pairs={{0,6},{2,0},{4,2},{6,4},{1,7},{3,1},{5,3},{7,5},{8,14},{10,8},{12,... | collective-permute-start | bytes 1572872 | tf_op jit(solution)/shard_map/ppermute | solution.py:18
  183.1 58.1 %collective-permute-start.13 = (bf16[1024,256]{1,0:T(8,128)(2,1)}, bf16[1024,256]{1,0:T(8,128)(2,1)}, u32[]{:S(2)}, u32[]{:S(2)}) collective-permute-start(bf16[1024,256]{1,0:T(8,128)(2,1)} %get-tuple-element.10.refs_0_), channel_id=1, source_target_pairs={{0,6},{2,0},{4,2},{6,4},{1,7},{3,1},{5,3},{7,5},{8,14},{10,8},{12,... | collective-permute-start | bytes 1572872 | tf_op jit(solution)/shard_map/ppermute | solution.py:18
  223.6 17.6 %copy-start.2 = (bf16[1024,256]{1,0:T(8,128)(2,1)}, bf16[1024,256]{1,0:T(8,128)(2,1)S(1)}, u32[]{:S(2)}) copy-start(bf16[1024,256]{1,0:T(8,128)(2,1)S(1)} %collective-permute-done.2.refs_3_) | copy-start | bytes 1572868
  223.6 19.5 %collective-permute-start.15 = (bf16[1024,256]{1,0:T(8,128)(2,1)}, bf16[1024,256]{1,0:T(8,128)(2,1)}, u32[]{:S(2)}, u32[]{:S(2)}) collective-permute-start(bf16[1024,256]{1,0:T(8,128)(2,1)} %get-tuple-element.11.refs_6_), channel_id=1, source_target_pairs={{0,2},{2,4},{4,6},{6,0},{1,3},{3,5},{5,7},{7,1},{8,10},{10,12},{12... | collective-permute-start | bytes 1572872 | tf_op jit(solution)/shard_map/ppermute | solution.py:18
  234.4 16.1 %collective-permute-start.3 = (bf16[1024,256]{1,0:T(8,128)(2,1)S(1)}, bf16[1024,256]{1,0:T(8,128)(2,1)}, u32[]{:S(2)}, u32[]{:S(2)}) collective-permute-start(bf16[1024,256]{1,0:T(8,128)(2,1)S(1)} %collective-permute-done.2.refs_3_), channel_id=1, source_target_pairs={{0,2},{2,4},{4,6},{6,0},{1,3},{3,5},{5,7},{7,1},{8,10},{10,12},{12... | collective-permute-start | bytes 1572872 | tf_op jit(solution)/shard_map/ppermute | solution.py:18
  235.4 7.7 %copy-start.3 = (bf16[1024,256]{1,0:T(8,128)(2,1)}, bf16[1024,256]{1,0:T(8,128)(2,1)S(1)}, u32[]{:S(2)}) copy-start(bf16[1024,256]{1,0:T(8,128)(2,1)S(1)} %collective-permute-done.refs_1_) | copy-start | bytes 1572868
  235.4 15.1 %collective-permute-start.8 = (bf16[1024,256]{1,0:T(8,128)(2,1)}, bf16[1024,256]{1,0:T(8,128)(2,1)}, u32[]{:S(2)}, u32[]{:S(2)}) collective-permute-start(bf16[1024,256]{1,0:T(8,128)(2,1)} %collective-permute-done.7.refs_9_), channel_id=1, source_target_pairs={{0,6},{2,0},{4,2},{6,4},{1,7},{3,1},{5,3},{7,5},{8,14},{10,8},{12,... | collective-permute-start | bytes 1572872 | tf_op jit(solution)/shard_map/ppermute | solution.py:18
  237.7 24.1 %collective-permute-start.14 = (bf16[1024,256]{1,0:T(8,128)(2,1)S(1)}, bf16[1024,256]{1,0:T(8,128)(2,1)}, u32[]{:S(2)}, u32[]{:S(2)}) collective-permute-start(bf16[1024,256]{1,0:T(8,128)(2,1)S(1)} %collective-permute-done.2.refs_3_), channel_id=1, source_target_pairs={{0,6},{2,0},{4,2},{6,4},{1,7},{3,1},{5,3},{7,5},{8,14},{10,8},{12,... | collective-permute-start | bytes 1572872 | tf_op jit(solution)/shard_map/ppermute | solution.py:18
  241.2 30.7 %collective-permute-start.16 = (bf16[1024,256]{1,0:T(8,128)(2,1)}, bf16[1024,256]{1,0:T(8,128)(2,1)}, u32[]{:S(2)}, u32[]{:S(2)}) collective-permute-start(bf16[1024,256]{1,0:T(8,128)(2,1)} %collective-permute-done.7.refs_9_), channel_id=1, source_target_pairs={{0,2},{2,4},{4,6},{6,0},{1,3},{3,5},{5,7},{7,1},{8,10},{10,12},{12... | collective-permute-start | bytes 1572872 | tf_op jit(solution)/shard_map/ppermute | solution.py:18
  243.2 42.1 %collective-permute-start.1 = (bf16[1024,256]{1,0:T(8,128)(2,1)S(1)}, bf16[1024,256]{1,0:T(8,128)(2,1)}, u32[]{:S(2)}, u32[]{:S(2)}) collective-permute-start(bf16[1024,256]{1,0:T(8,128)(2,1)S(1)} %collective-permute-done.refs_1_), channel_id=1, source_target_pairs={{0,2},{2,4},{4,6},{6,0},{1,3},{3,5},{5,7},{7,1},{8,10},{10,12},{12... | collective-permute-start | bytes 1572872 | tf_op jit(solution)/shard_map/ppermute | solution.py:18
  250.5 34.8 %collective-permute-start.6 = (bf16[1024,256]{1,0:T(8,128)(2,1)}, bf16[1024,256]{1,0:T(8,128)(2,1)}, u32[]{:S(2)}, u32[]{:S(2)}) collective-permute-start(bf16[1024,256]{1,0:T(8,128)(2,1)} %collective-permute-done.5.refs_8_), channel_id=1, source_target_pairs={{0,6},{2,0},{4,2},{6,4},{1,7},{3,1},{5,3},{7,5},{8,14},{10,8},{12,... | collective-permute-start | bytes 1572872 | tf_op jit(solution)/shard_map/ppermute | solution.py:18
  250.5 34.8 %collective-permute-start.4 = (bf16[1024,256]{1,0:T(8,128)(2,1)}, bf16[1024,256]{1,0:T(8,128)(2,1)}, u32[]{:S(2)}, u32[]{:S(2)}) collective-permute-start(bf16[1024,256]{1,0:T(8,128)(2,1)} %collective-permute-done.3.refs_4_), channel_id=1, source_target_pairs={{0,2},{2,4},{4,6},{6,0},{1,3},{3,5},{5,7},{7,1},{8,10},{10,12},{12... | collective-permute-start | bytes 1572872 | tf_op jit(solution)/shard_map/ppermute | solution.py:18
  261.8 23.6 %collective-permute-start.9 = (bf16[1024,256]{1,0:T(8,128)(2,1)}, bf16[1024,256]{1,0:T(8,128)(2,1)S(1)}, u32[]{:S(2)}, u32[]{:S(2)}) collective-permute-start(bf16[1024,256]{1,0:T(8,128)(2,1)} %collective-permute-done.8.refs_11_), channel_id=1, source_target_pairs={{0,6},{2,0},{4,2},{6,4},{1,7},{3,1},{5,3},{7,5},{8,14},{10,8},{12,... | collective-permute-start | bytes 1572872 | tf_op jit(solution)/shard_map/ppermute | solution.py:18
  285.3 0.8 copy-start.4
where the time goes:
time: 297 us; the launch traced here: 296 us
  Pallas kernels  159 us (54%)
  waiting for transfers between devices  76.5 us (26%)
  starting transfers between devices  45.9 us (15%)
  matrix products  10.2 us (3%)
  other arithmetic  3.84 us (1%)
    pallas_call x2, Pallas kernels, packed(): pl.pallas_call(kernel, in_specs=[pl.BlockSpec(memory_space=pl.ANY)], out_...  129 us
    ppermute x17, waiting for transfers between devices, shift(): lax.ppermute(value, axis, [(i, (i + step) % size) for i in range(size)])  71.9 us
    pallas_call x2, Pallas kernels, combined(): pl.pallas_call(kernel, grid_spec=pltpu.PrefetchScalarGridSpec(num_scalar_...  23.3 us
    ppermute x17, starting transfers between devices, shift(): lax.ppermute(value, axis, [(i, (i + step) % size) for i in range(size)])  23.1 us
    all_to_all x3, starting transfers between devices, exchange(): return lax.all_to_all(value, axes, split_axis=0, concat_axis=0, tiled=True)  22.8 us
    dot_general x1, matrix products, body(): jnp.dot(rest.reshape(-1, width), right, preferred_element_type=F32)  6.72 us
    pallas_call x1, Pallas kernels, left_applied(): pl.pallas_call(kernel, grid=(2,), in_specs=[pl.BlockSpec((half, order), l...  6.17 us
  transfers between devices with their start and end apart: 20, of which 7 were waited for; matrix products, arithmetic and copies ran while one was open for 5% of the time, Pallas kernels for 50%

commit v1 on v0

--- a/solution.py
+++ b/solution.py
@@ -25,63 +25,72 @@
 def packed(cotangents, steps, groups, width):
     rows = cotangents.shape[0]
     z_size = lax.axis_size("z")
+    pieces = len(steps) * groups
 
     def kernel(source, *refs):
-        targets, semaphore = refs[:-1], refs[-1]
+        targets, (space, arrived, left) = refs[:-3], refs[-3:]
         z = lax.axis_index("z")
-        copies = []
-        for target, step in zip(targets, steps):
-            first = ((z + step) % z_size) * (groups * width)
-            for g in range(groups):
-                copies.append(
-                    pltpu.make_async_copy(
-                        source.at[:, pl.ds(pl.multiple_of(first + g * width, width), width)],
-                        target.at[g],
-                        semaphore.at[len(copies)],
-                    )
-                )
-        for copy in copies:
-            copy.start()
-        for copy in copies:
-            copy.wait()
+        loads, stores = [], []
+        for k in range(pieces):
+            first = (((z + steps[k // groups]) % z_size) * groups + k % groups) * width
+            columns = pl.ds(pl.multiple_of(first, width), width)
+            loads.append(pltpu.make_async_copy(source.at[:, columns], space.at[k], arrived.at[k]))
+            stores.append(pltpu.make_async_copy(space.at[k], targets[k // groups].at[k % groups], left.at[k]))
+        for load in loads:
+            load.start()
+        for load, store in zip(loads, stores):
+            load.wait()
+            store.start()
+        for store in stores:
+            store.wait()
 
     return pl.pallas_call(
         kernel,
-        in_specs=[pl.BlockSpec(memory_space=pl.ANY)],
-        out_specs=[pl.BlockSpec(memory_space=pl.ANY)] * len(steps),
-        out_shape=[jax.ShapeDtypeStruct((groups, rows, width), cotangents.dtype)] * len(steps),
-        scratch_shapes=[pltpu.SemaphoreType.DMA((len(steps) * groups,))],
+        in_specs=[pl.BlockSpec(memory_space=pltpu.HBM)],
+        out_specs=[pl.BlockSpec(memory_space=pltpu.HBM)] * len(steps),
+        out_shape=[pltpu.HBM((groups, rows, width), cotangents.dtype)] * len(steps),
+        scratch_shapes=[
+            pltpu.VMEM((pieces, rows, width), cotangents.dtype),
+            pltpu.SemaphoreType.DMA((pieces,)),
+            pltpu.SemaphoreType.DMA((pieces,)),
+        ],
+        compiler_params=pltpu.CompilerParams(vmem_limit_bytes=8 << 20),
         name="packed",
-    )(cotangents)
+    )(pltpu.with_memory_space_constraint(cotangents, pltpu.HBM))
 
 
 def left_applied(left, tokens):
     order, count = left.shape[0], tokens.shape[0]
     half = order // 2
+    tile = 512
+    steps = half // tile
 
     def kernel(left_ref, tokens_ref, low_ref, high_ref):
         value = lax.dot_general(
             left_ref[...], tokens_ref[...], (((1,), (1,)), ((), ())), preferred_element_type=F32
         ).astype(BF16)
 
-        @pl.when(pl.program_id(0) == 0)
+        @pl.when(pl.program_id(0) < steps)
         def _():
             low_ref[...] = value
 
-        @pl.when(pl.program_id(0) == 1)
+        @pl.when(pl.program_id(0) >= steps)
         def _():
             high_ref[...] = value
 
     return pl.pallas_call(
         kernel,
-        grid=(2,),
+        grid=(2 * steps,),
         in_specs=[
-            pl.BlockSpec((half, order), lambda i: (i, 0)),
+            pl.BlockSpec((tile, order), lambda i: (i, 0)),
             pl.BlockSpec((count, order), lambda i: (0, 0)),
         ],
-        out_specs=[pl.BlockSpec((half, count), lambda i: (0, 0))] * 2,
+        out_specs=[
+            pl.BlockSpec((tile, count), lambda i: (jnp.minimum(i, steps - 1), 0)),
+            pl.BlockSpec((tile, count), lambda i: (jnp.maximum(i - steps, 0), 0)),
+        ],
         out_shape=[jax.ShapeDtypeStruct((half, count), BF16)] * 2,
-        compiler_params=pltpu.CompilerParams(dimension_semantics=("arbitrary",)),
+        compiler_params=pltpu.CompilerParams(dimension_semantics=("arbitrary",), vmem_limit_bytes=16 << 20),
         name="left_applied",
     )(left, tokens)
 
@@ -89,7 +98,7 @@
 def combined(side, lows, highs, rights, base, out_type):
     half, count = lows[0].shape
     width = rights[0][0].shape[-1]
-    tile = 256
+    tile = 512
     steps = half // tile
     pieces = len(lows)
 
@@ -135,7 +144,7 @@
             out_specs=row_spec,
         ),
         out_shape=jax.ShapeDtypeStruct((2 * half, width), out_type),
-        compiler_params=pltpu.CompilerParams(dimension_semantics=("arbitrary",)),
+        compiler_params=pltpu.CompilerParams(dimension_semantics=("arbitrary",), vmem_limit_bytes=30 << 20),
         name="combined",
     )(side.reshape(1), *lows, *highs, *[r[0] for r in rights], *bases)
 

time: 297 us -> 191 us (0.64)
  Pallas kernels: 159 us -> 24 us
  waiting for transfers between devices: 76.5 us -> 103 us
    pallas_call x3, Pallas kernels: 135 us -> 8.78 us  [the longest x2 4.83 us: packed(): pl.pallas_call(kernel, in_specs=[pl.BlockSpec(memory_space=pltpu.HBM)], o...]
    ppermute x17, waiting for transfers between devices: 71.9 us -> 101 us  [shift(): lax.ppermute(value, axis, [(i, (i + step) % size) for i in range(size)])]
    pallas_call x2, Pallas kernels: 23.3 us -> 15.2 us  [combined(): pl.pallas_call(kernel, grid_spec=pltpu.PrefetchScalarGridSpec(num_scalar_...]
  transfers between devices with their start and end apart: 20 -> 20, of which waited for: 7 -> 9; matrix products, arithmetic and copies ran while one was open for 5% -> 6% of each run, Pallas kernels for 50% -> 10%
where the time goes in v1:
time: 191 us; the launch traced here: 190 us
  waiting for transfers between devices  103 us (54%)
  starting transfers between devices  48.1 us (25%)
  Pallas kernels  24 us (13%)
  matrix products  8 us (4%)
  other arithmetic  3.84 us (2%)
  local copies, waits for them, and re-layouts  3.38 us (2%)
    ppermute x17, waiting for transfers between devices, shift(): lax.ppermute(value, axis, [(i, (i + step) % size) for i in range(size)])  101 us
    all_to_all x3, starting transfers between devices, exchange(): return lax.all_to_all(value, axes, split_axis=0, concat_axis=0, tiled=True)  24.3 us
    ppermute x17, starting transfers between devices, shift(): lax.ppermute(value, axis, [(i, (i + step) % size) for i in range(size)])  23.8 us
    pallas_call x2, Pallas kernels, combined(): pl.pallas_call(kernel, grid_spec=pltpu.PrefetchScalarGridSpec(num_scalar_...  15.2 us
    dot_general x1, matrix products, body(): jnp.dot(rest.reshape(-1, width), right, preferred_element_type=F32)  5.53 us
    pallas_call x2, Pallas kernels, packed(): pl.pallas_call(kernel, in_specs=[pl.BlockSpec(memory_space=pltpu.HBM)], o...  4.83 us
    pallas_call x1, Pallas kernels, left_applied(): pl.pallas_call(kernel, grid=(2 * steps,), in_specs=[pl.BlockSpec((tile, o...  3.94 us
    another operation x1, other arithmetic, body(): rest = exchange(jnp.stack([up, down, far], axis=1), PLANE)  3.84 us
  transfers between devices with their start and end apart: 20, of which 9 were waited for; matrix products, arithmetic and copies ran while one was open for 6% of the time, Pallas kernels for 10%

profile of v1, /device:TPU:22, one launch (start us, length us, event | category | flops | bytes accessed | tf_op | source)
XLA Modules:
  0.0 190.2 jit_solution(13340012062968683816)
XLA Ops:
  0.0 7.4 %all-to-all-start = ((bf16[16,16,2048]{2,1,0:T(8,128)(2,1)}), bf16[16,16,2048]{2,1,0:T(8,128)(2,1)S(1)}, u32[]{:S(2)}, u32[]{:S(2)}) async-start(bf16[16,16,2048]{2,1,0:T(8,128)(2,1)} %bitcast.36), calls=%async_computation | async-start | bytes 2097152 | tf_op jit(solution)/shard_map/all_to_all | solution.py:22
  7.4 2.8 %packed.2 = (bf16[2,256,1024]{2,1,0:T(8,128)(2,1)}, bf16[2,256,1024]{2,1,0:T(8,128)(2,1)}, bf16[2,256,1024]{2,1,0:T(8,128)(2,1)}) custom-call(bf16[256,8192]{1,0:T(8,128)(2,1)} %source.3), custom_call_target="tpu_custom_call" | custom-call | tf_op jit(solution)/shard_map/packed/pallas_call | solution.py:47
  10.2 2.0 %collective-permute-start.10 = (bf16[32,16,1024]{2,1,0:T(8,128)(2,1)}, bf16[32,16,1024]{2,1,0:T(8,128)(2,1)}, u32[]{:S(2)}, u32[]{:S(2)}) collective-permute-start(bf16[32,16,1024]{2,1,0:T(8,128)(2,1)} %bitcast.39), channel_id=1, source_target_pairs={{0,2},{2,4},{4,6},{6,0},{1,3},{3,5},{5,7},{7,1},{8,10},{10,12},{12... | collective-permute-start | bytes 3145736 | tf_op jit(solution)/shard_map/ppermute | solution.py:18
  12.2 2.2 %collective-permute-start.11 = (bf16[32,16,1024]{2,1,0:T(8,128)(2,1)}, bf16[32,16,1024]{2,1,0:T(8,128)(2,1)}, u32[]{:S(2)}, u32[]{:S(2)}) collective-permute-start(bf16[32,16,1024]{2,1,0:T(8,128)(2,1)} %bitcast.38), channel_id=1, source_target_pairs={{0,6},{2,0},{4,2},{6,4},{1,7},{3,1},{5,3},{7,5},{8,14},{10,8},{12,... | collective-permute-start | bytes 3145736 | tf_op jit(solution)/shard_map/ppermute | solution.py:18
  14.4 1.8 collective-permute-start.12
  16.1 2.0 %packed.3 = bf16[2,256,1024]{2,1,0:T(8,128)(2,1)} custom-call(bf16[256,8192]{1,0:T(8,128)(2,1)} %source.3), custom_call_target="tpu_custom_call" | custom-call | tf_op jit(solution)/shard_map/packed/pallas_call | solution.py:47
  18.2 2.2 %all-to-all-done = bf16[16,16,2048]{2,1,0:T(8,128)(2,1)S(1)} async-done(((bf16[16,16,2048]{2,1,0:T(8,128)(2,1)}), bf16[16,16,2048]{2,1,0:T(8,128)(2,1)S(1)}, u32[]{:S(2)}, u32[]{:S(2)}) %all-to-all-start) | async-done | bytes 1048608 | tf_op jit(solution)/shard_map/all_to_all | solution.py:22
  20.4 9.5 %all-to-all-start.2 = ((bf16[32,16,1024]{2,1,0:T(8,128)(2,1)}), bf16[32,16,1024]{2,1,0:T(8,128)(2,1)}, u32[]{:S(2)}, u32[]{:S(2)}) async-start(bf16[32,16,1024]{2,1,0:T(8,128)(2,1)} %bitcast.35), calls=%async_computation.2 | async-start | bytes 2097152 | tf_op jit(solution)/shard_map/all_to_all | solution.py:22
  29.9 8.2 %collective-permute-done.10 = bf16[32,16,1024]{2,1,0:T(8,128)(2,1)} collective-permute-done((bf16[32,16,1024]{2,1,0:T(8,128)(2,1)}, bf16[32,16,1024]{2,1,0:T(8,128)(2,1)}, u32[]{:S(2)}, u32[]{:S(2)}) %collective-permute-start.10) | collective-permute-done | bytes 1048608 | tf_op jit(solution)/shard_map/ppermute | solution.py:18
  38.0 21.8 %collective-permute-done.11 = bf16[32,16,1024]{2,1,0:T(8,128)(2,1)} collective-permute-done((bf16[32,16,1024]{2,1,0:T(8,128)(2,1)}, bf16[32,16,1024]{2,1,0:T(8,128)(2,1)}, u32[]{:S(2)}, u32[]{:S(2)}) %collective-permute-start.11) | collective-permute-done | bytes 1048608 | tf_op jit(solution)/shard_map/ppermute | solution.py:18
  59.9 1.8 collective-permute-done.12
  61.7 3.8 %pad_maximum_fusion = bf16[32,3,16,1024]{3,2,1,0:T(8,128)(2,1)} fusion(bf16[32,1,16,1024]{3,2,1,0:T(8,128)(2,1)} %bitcast.9, bf16[32,1,16,1024]{3,2,1,0:T(8,128)(2,1)} %bitcast.7, bf16[32,1,16,1024]{3,2,1,0:T(8,128)(2,1)} %bitcast.5), kind=kLoop, calls=%fused_computation.1 | loop fusion | flops 3145728 | bytes 6291456 | tf_op jit(solution)/shard_map/stack | solution.py:172
  65.5 0.0 all-to-all-done.2
  65.5 7.4 %all-to-all-start.1 = ((bf16[32,3,16,1024]{3,2,1,0:T(8,128)(2,1)}), bf16[32,3,16,1024]{3,2,1,0:T(8,128)(2,1)}, u32[]{:S(2)}, u32[]{:S(2)}) async-start(bf16[32,3,16,1024]{3,2,1,0:T(8,128)(2,1)} %pad_maximum_fusion), calls=%async_computation.1 | async-start | bytes 6291456 | tf_op jit(solution)/shard_map/all_to_all | solution.py:22
  73.0 0.0 copy-start.1
  73.0 3.4 %copy-done.1 = bf16[1,2048,2048]{2,1,0:T(8,128)(2,1)S(1)} copy-done((bf16[1,2048,2048]{2,1,0:T(8,128)(2,1)S(1)}, bf16[1,2048,2048]{2,1,0:T(8,128)(2,1)}, u32[]{:S(2)}) %copy-start.1) | copy-done | bytes 8388632
  76.4 3.9 %left_applied.1 = (bf16[1024,256]{1,0:T(8,128)(2,1)}, bf16[1024,256]{1,0:T(8,128)(2,1)}) custom-call(bf16[2048,2048]{1,0:T(8,128)(2,1)S(1)} %bitcast.31, bf16[256,2048]{1,0:T(8,128)(2,1)S(1)} %bitcast.34), custom_call_target="tpu_custom_call" | custom-call | tf_op jit(solution)/shard_map/left_applied/pallas_call | solution.py:81
  80.3 0.8 collective-permute-start.2
  81.1 1.2 collective-permute-start.7
  82.3 1.1 collective-permute-start
  83.5 2.1 %collective-permute-start.5 = (bf16[1024,256]{1,0:T(8,128)(2,1)}, bf16[1024,256]{1,0:T(8,128)(2,1)}, u32[]{:S(2)}, u32[]{:S(2)}) collective-permute-start(bf16[1024,256]{1,0:T(8,128)(2,1)} %get-tuple-element.11.refs_6_), channel_id=1, source_target_pairs={{0,6},{2,0},{4,2},{6,4},{1,7},{3,1},{5,3},{7,5},{8,14},{10,8},{12,... | collective-permute-start | bytes 1572872 | tf_op jit(solution)/shard_map/ppermute | solution.py:18
  85.6 0.7 collective-permute-start.13
  86.2 38.9 %collective-permute-done.2.refs_3_ = bf16[1024,256]{1,0:T(8,128)(2,1)} collective-permute-done((bf16[1024,256]{1,0:T(8,128)(2,1)}, bf16[1024,256]{1,0:T(8,128)(2,1)}, u32[]{:S(2)}, u32[]{:S(2)}) %collective-permute-start.2) | collective-permute-done | bytes 524320 | tf_op jit(solution)/shard_map/ppermute | solution.py:18
  125.1 1.1 collective-permute-start.15
  126.2 9.5 %collective-permute-done.7.refs_9_ = bf16[1024,256]{1,0:T(8,128)(2,1)} collective-permute-done((bf16[1024,256]{1,0:T(8,128)(2,1)}, bf16[1024,256]{1,0:T(8,128)(2,1)}, u32[]{:S(2)}, u32[]{:S(2)}) %collective-permute-start.7) | collective-permute-done | bytes 524320 | tf_op jit(solution)/shard_map/ppermute | solution.py:18
  135.8 1.1 collective-permute-start.3
  136.9 0.0 collective-permute-done.refs_1_
  136.9 2.1 %collective-permute-start.8 = (bf16[1024,256]{1,0:T(8,128)(2,1)}, bf16[1024,256]{1,0:T(8,128)(2,1)}, u32[]{:S(2)}, u32[]{:S(2)}) collective-permute-start(bf16[1024,256]{1,0:T(8,128)(2,1)} %collective-permute-done.7.refs_9_), channel_id=1, source_target_pairs={{0,6},{2,0},{4,2},{6,4},{1,7},{3,1},{5,3},{7,5},{8,14},{10,8},{12,... | collective-permute-start | bytes 1572872 | tf_op jit(solution)/shard_map/ppermute | solution.py:18
  139.0 0.0 collective-permute-done.5.refs_8_
  139.0 0.7 collective-permute-start.14
  139.6 2.5 %fusion.3 = bf16[512,1024]{1,0:T(8,128)(2,1)S(1)} fusion(bf16[512,1024]{1,0:T(8,128)(2,1)} %bitcast.14, bf16[1,1,1024,1024]{3,2,1,0:T(8,128)(2,1)S(1)} %copy-done), kind=kOutput, calls=%fused_computation.5 | convolution fusion | flops 1074266112 | bytes 4194304 | tf_op jit(solution)/shard_map/dot_general | solution.py:182
  142.1 0.0 collective-permute-done.13.refs_2_
  142.1 1.4 collective-permute-start.16
  143.6 0.0 collective-permute-done.15.refs_7_
  143.6 0.1 collective-permute-start.1
  143.7 8.4 %collective-permute-done.3.refs_4_ = bf16[1024,256]{1,0:T(8,128)(2,1)} collective-permute-done((bf16[1024,256]{1,0:T(8,128)(2,1)}, bf16[1024,256]{1,0:T(8,128)(2,1)}, u32[]{:S(2)}, u32[]{:S(2)}) %collective-permute-start.3) | collective-permute-done | bytes 524320 | tf_op jit(solution)/shard_map/ppermute | solution.py:18
  152.1 0.7 collective-permute-start.6
  152.7 0.0 collective-permute-done.8.refs_11_
  152.7 1.4 collective-permute-start.4
  154.1 9.1 %collective-permute-done.14.refs_5_ = bf16[1024,256]{1,0:T(8,128)(2,1)} collective-permute-done((bf16[1024,256]{1,0:T(8,128)(2,1)}, bf16[1024,256]{1,0:T(8,128)(2,1)}, u32[]{:S(2)}, u32[]{:S(2)}) %collective-permute-start.14) | collective-permute-done | bytes 524320 | tf_op jit(solution)/shard_map/ppermute | solution.py:18
  163.2 3.3 %collective-permute-start.9 = (bf16[1024,256]{1,0:T(8,128)(2,1)}, bf16[1024,256]{1,0:T(8,128)(2,1)}, u32[]{:S(2)}, u32[]{:S(2)}) collective-permute-start(bf16[1024,256]{1,0:T(8,128)(2,1)} %collective-permute-done.8.refs_11_), channel_id=1, source_target_pairs={{0,6},{2,0},{4,2},{6,4},{1,7},{3,1},{5,3},{7,5},{8,14},{10,8},{12,... | collective-permute-start | bytes 1572872 | tf_op jit(solution)/shard_map/ppermute | solution.py:18
  166.5 0.0 all-to-all-done.1
  166.6 5.5 %convolution_convert_fusion = bf16[1536,1024]{1,0:T(8,128)(2,1)S(1)} fusion(bf16[1536,1024]{1,0:T(8,128)(2,1)} %bitcast.10, bf16[1,1,1024,1024]{3,2,1,0:T(8,128)(2,1)S(1)} %copy-done), kind=kOutput, calls=%fused_computation | convolution fusion | flops 3222798336 | bytes 8388608 | tf_op jit(solution)/shard_map/dot_general | solution.py:183
  172.1 9.4 %combined.2.refs_6_ = f32[2048,1024]{1,0:T(8,128)S(1)} custom-call(s32[1]{0:T(128)} %bitcast.side_ref, bf16[1024,256]{1,0:T(8,128)(2,1)} %get-tuple-element.10.refs_0_, bf16[1024,256]{1,0:T(8,128)(2,1)} %collective-permute-done.refs_1_, bf16[1024,256]{1,0:T(8,128)(2,1)} %collective-permute-done.13.refs_2_, bf16[1024,256]{1,0:T(8,128)(2,1)} %collective-permute-done.2.refs_3_, ...), custom_call_target="tpu_custom_call" | custom-call | tf_op jit(solution)/shard_map/combined/pallas_call | solution.py:138
  181.5 0.0 collective-permute-done.1.refs_0_
  181.5 2.9 %collective-permute-done.4.refs_1_ = bf16[1024,256]{1,0:T(8,128)(2,1)} collective-permute-done((bf16[1024,256]{1,0:T(8,128)(2,1)}, bf16[1024,256]{1,0:T(8,128)(2,1)}, u32[]{:S(2)}, u32[]{:S(2)}) %collective-permute-start.4) | collective-permute-done | bytes 524320 | tf_op jit(solution)/shard_map/ppermute | solution.py:18
  184.3 0.0 collective-permute-done.9.refs_3_
  184.3 5.8 %combined.3 = bf16[2048,1024]{1,0:T(8,128)(2,1)} custom-call(s32[1]{0:T(128)} %bitcast.side_ref, bf16[1024,256]{1,0:T(8,128)(2,1)} %collective-permute-done.1.refs_0_, bf16[1024,256]{1,0:T(8,128)(2,1)} %collective-permute-done.4.refs_1_, bf16[1024,256]{1,0:T(8,128)(2,1)} %collective-permute-done.6.refs_2_, bf16[1024,256]{1,0:T(8,128)(2,1)} %collective-permute-done.9.refs_3_, ...), custom_call_target="tpu_custom_call" | custom-call | tf_op jit(solution)/shard_map/combined/pallas_call | solution.py:138
  (4 shorter events, 0.0 us)
Async XLA Ops:
  0.0 139.6 %copy-start = (bf16[1,1,1024,1024]{3,2,1,0:T(8,128)(2,1)S(1)}, bf16[1,1,1024,1024]{3,2,1,0:T(8,128)(2,1)}, u32[]{:S(2)}) copy-start(bf16[1,1,1024,1024]{3,2,1,0:T(8,128)(2,1)} %param.7) | copy-start | bytes 6291460
  0.0 20.4 %all-to-all-start = ((bf16[16,16,2048]{2,1,0:T(8,128)(2,1)}), bf16[16,16,2048]{2,1,0:T(8,128)(2,1)S(1)}, u32[]{:S(2)}, u32[]{:S(2)}) async-start(bf16[16,16,2048]{2,1,0:T(8,128)(2,1)} %bitcast.36), calls=%async_computation | async-start | bytes 2097152 | tf_op jit(solution)/shard_map/all_to_all | solution.py:22
  10.2 27.9 %collective-permute-start.10 = (bf16[32,16,1024]{2,1,0:T(8,128)(2,1)}, bf16[32,16,1024]{2,1,0:T(8,128)(2,1)}, u32[]{:S(2)}, u32[]{:S(2)}) collective-permute-start(bf16[32,16,1024]{2,1,0:T(8,128)(2,1)} %bitcast.39), channel_id=1, source_target_pairs={{0,2},{2,4},{4,6},{6,0},{1,3},{3,5},{5,7},{7,1},{8,10},{10,12},{12... | collective-permute-start | bytes 3145736 | tf_op jit(solution)/shard_map/ppermute | solution.py:18
  12.2 47.7 %collective-permute-start.11 = (bf16[32,16,1024]{2,1,0:T(8,128)(2,1)}, bf16[32,16,1024]{2,1,0:T(8,128)(2,1)}, u32[]{:S(2)}, u32[]{:S(2)}) collective-permute-start(bf16[32,16,1024]{2,1,0:T(8,128)(2,1)} %bitcast.38), channel_id=1, source_target_pairs={{0,6},{2,0},{4,2},{6,4},{1,7},{3,1},{5,3},{7,5},{8,14},{10,8},{12,... | collective-permute-start | bytes 3145736 | tf_op jit(solution)/shard_map/ppermute | solution.py:18
  14.4 47.3 %collective-permute-start.12 = (bf16[32,16,1024]{2,1,0:T(8,128)(2,1)}, bf16[32,16,1024]{2,1,0:T(8,128)(2,1)}, u32[]{:S(2)}, u32[]{:S(2)}) collective-permute-start(bf16[32,16,1024]{2,1,0:T(8,128)(2,1)} %bitcast.37), channel_id=1, source_target_pairs={{0,4},{2,6},{4,0},{6,2},{1,5},{3,7},{5,1},{7,3},{8,12},{10,14},{12... | collective-permute-start | bytes 3145736 | tf_op jit(solution)/shard_map/ppermute | solution.py:18
  20.4 45.2 %all-to-all-start.2 = ((bf16[32,16,1024]{2,1,0:T(8,128)(2,1)}), bf16[32,16,1024]{2,1,0:T(8,128)(2,1)}, u32[]{:S(2)}, u32[]{:S(2)}) async-start(bf16[32,16,1024]{2,1,0:T(8,128)(2,1)} %bitcast.35), calls=%async_computation.2 | async-start | bytes 2097152 | tf_op jit(solution)/shard_map/all_to_all | solution.py:22
  65.5 101.0 %all-to-all-start.1 = ((bf16[32,3,16,1024]{3,2,1,0:T(8,128)(2,1)}), bf16[32,3,16,1024]{3,2,1,0:T(8,128)(2,1)}, u32[]{:S(2)}, u32[]{:S(2)}) async-start(bf16[32,3,16,1024]{3,2,1,0:T(8,128)(2,1)} %pad_maximum_fusion), calls=%async_computation.1 | async-start | bytes 6291456 | tf_op jit(solution)/shard_map/all_to_all | solution.py:22
  73.0 3.4 %copy-start.1 = (bf16[1,2048,2048]{2,1,0:T(8,128)(2,1)S(1)}, bf16[1,2048,2048]{2,1,0:T(8,128)(2,1)}, u32[]{:S(2)}) copy-start(bf16[1,2048,2048]{2,1,0:T(8,128)(2,1)} %param.6) | copy-start | bytes 25165828
  80.3 44.8 %collective-permute-start.2 = (bf16[1024,256]{1,0:T(8,128)(2,1)}, bf16[1024,256]{1,0:T(8,128)(2,1)}, u32[]{:S(2)}, u32[]{:S(2)}) collective-permute-start(bf16[1024,256]{1,0:T(8,128)(2,1)} %get-tuple-element.10.refs_0_), channel_id=1, source_target_pairs={{0,1},{1,0},{2,3},{3,2},{4,5},{5,4},{6,7},{7,6},{8,9},{9,8},{10,11... | collective-permute-start | bytes 1572872 | tf_op jit(solution)/shard_map/ppermute | solution.py:18
  81.1 54.6 %collective-permute-start.7 = (bf16[1024,256]{1,0:T(8,128)(2,1)}, bf16[1024,256]{1,0:T(8,128)(2,1)}, u32[]{:S(2)}, u32[]{:S(2)}) collective-permute-start(bf16[1024,256]{1,0:T(8,128)(2,1)} %get-tuple-element.11.refs_6_), channel_id=1, source_target_pairs={{0,1},{1,0},{2,3},{3,2},{4,5},{5,4},{6,7},{7,6},{8,9},{9,8},{10,11... | collective-permute-start | bytes 1572872 | tf_op jit(solution)/shard_map/ppermute | solution.py:18
  82.3 54.6 %collective-permute-start = (bf16[1024,256]{1,0:T(8,128)(2,1)}, bf16[1024,256]{1,0:T(8,128)(2,1)}, u32[]{:S(2)}, u32[]{:S(2)}) collective-permute-start(bf16[1024,256]{1,0:T(8,128)(2,1)} %get-tuple-element.10.refs_0_), channel_id=1, source_target_pairs={{0,2},{2,4},{4,6},{6,0},{1,3},{3,5},{5,7},{7,1},{8,10},{10,12},{12... | collective-permute-start | bytes 1572872 | tf_op jit(solution)/shard_map/ppermute | solution.py:18
  83.5 55.5 %collective-permute-start.5 = (bf16[1024,256]{1,0:T(8,128)(2,1)}, bf16[1024,256]{1,0:T(8,128)(2,1)}, u32[]{:S(2)}, u32[]{:S(2)}) collective-permute-start(bf16[1024,256]{1,0:T(8,128)(2,1)} %get-tuple-element.11.refs_6_), channel_id=1, source_target_pairs={{0,6},{2,0},{4,2},{6,4},{1,7},{3,1},{5,3},{7,5},{8,14},{10,8},{12,... | collective-permute-start | bytes 1572872 | tf_op jit(solution)/shard_map/ppermute | solution.py:18
  85.6 56.6 %collective-permute-start.13 = (bf16[1024,256]{1,0:T(8,128)(2,1)}, bf16[1024,256]{1,0:T(8,128)(2,1)}, u32[]{:S(2)}, u32[]{:S(2)}) collective-permute-start(bf16[1024,256]{1,0:T(8,128)(2,1)} %get-tuple-element.10.refs_0_), channel_id=1, source_target_pairs={{0,6},{2,0},{4,2},{6,4},{1,7},{3,1},{5,3},{7,5},{8,14},{10,8},{12,... | collective-permute-start | bytes 1572872 | tf_op jit(solution)/shard_map/ppermute | solution.py:18
  125.1 18.5 %collective-permute-start.15 = (bf16[1024,256]{1,0:T(8,128)(2,1)}, bf16[1024,256]{1,0:T(8,128)(2,1)}, u32[]{:S(2)}, u32[]{:S(2)}) collective-permute-start(bf16[1024,256]{1,0:T(8,128)(2,1)} %get-tuple-element.11.refs_6_), channel_id=1, source_target_pairs={{0,2},{2,4},{4,6},{6,0},{1,3},{3,5},{5,7},{7,1},{8,10},{10,12},{12... | collective-permute-start | bytes 1572872 | tf_op jit(solution)/shard_map/ppermute | solution.py:18
  135.8 16.3 %collective-permute-start.3 = (bf16[1024,256]{1,0:T(8,128)(2,1)}, bf16[1024,256]{1,0:T(8,128)(2,1)}, u32[]{:S(2)}, u32[]{:S(2)}) collective-permute-start(bf16[1024,256]{1,0:T(8,128)(2,1)} %collective-permute-done.2.refs_3_), channel_id=1, source_target_pairs={{0,2},{2,4},{4,6},{6,0},{1,3},{3,5},{5,7},{7,1},{8,10},{10,12},{12... | collective-permute-start | bytes 1572872 | tf_op jit(solution)/shard_map/ppermute | solution.py:18
  136.9 15.8 %collective-permute-start.8 = (bf16[1024,256]{1,0:T(8,128)(2,1)}, bf16[1024,256]{1,0:T(8,128)(2,1)}, u32[]{:S(2)}, u32[]{:S(2)}) collective-permute-start(bf16[1024,256]{1,0:T(8,128)(2,1)} %collective-permute-done.7.refs_9_), channel_id=1, source_target_pairs={{0,6},{2,0},{4,2},{6,4},{1,7},{3,1},{5,3},{7,5},{8,14},{10,8},{12,... | collective-permute-start | bytes 1572872 | tf_op jit(solution)/shard_map/ppermute | solution.py:18
  139.0 24.2 %collective-permute-start.14 = (bf16[1024,256]{1,0:T(8,128)(2,1)}, bf16[1024,256]{1,0:T(8,128)(2,1)}, u32[]{:S(2)}, u32[]{:S(2)}) collective-permute-start(bf16[1024,256]{1,0:T(8,128)(2,1)} %collective-permute-done.2.refs_3_), channel_id=1, source_target_pairs={{0,6},{2,0},{4,2},{6,4},{1,7},{3,1},{5,3},{7,5},{8,14},{10,8},{12,... | collective-permute-start | bytes 1572872 | tf_op jit(solution)/shard_map/ppermute | solution.py:18
  142.1 29.9 %collective-permute-start.16 = (bf16[1024,256]{1,0:T(8,128)(2,1)}, bf16[1024,256]{1,0:T(8,128)(2,1)}, u32[]{:S(2)}, u32[]{:S(2)}) collective-permute-start(bf16[1024,256]{1,0:T(8,128)(2,1)} %collective-permute-done.7.refs_9_), channel_id=1, source_target_pairs={{0,2},{2,4},{4,6},{6,0},{1,3},{3,5},{5,7},{7,1},{8,10},{10,12},{12... | collective-permute-start | bytes 1572872 | tf_op jit(solution)/shard_map/ppermute | solution.py:18
  143.6 37.9 %collective-permute-start.1 = (bf16[1024,256]{1,0:T(8,128)(2,1)}, bf16[1024,256]{1,0:T(8,128)(2,1)}, u32[]{:S(2)}, u32[]{:S(2)}) collective-permute-start(bf16[1024,256]{1,0:T(8,128)(2,1)} %collective-permute-done.refs_1_), channel_id=1, source_target_pairs={{0,2},{2,4},{4,6},{6,0},{1,3},{3,5},{5,7},{7,1},{8,10},{10,12},{12... | collective-permute-start | bytes 1572872 | tf_op jit(solution)/shard_map/ppermute | solution.py:18
  152.1 29.4 %collective-permute-start.6 = (bf16[1024,256]{1,0:T(8,128)(2,1)}, bf16[1024,256]{1,0:T(8,128)(2,1)}, u32[]{:S(2)}, u32[]{:S(2)}) collective-permute-start(bf16[1024,256]{1,0:T(8,128)(2,1)} %collective-permute-done.5.refs_8_), channel_id=1, source_target_pairs={{0,6},{2,0},{4,2},{6,4},{1,7},{3,1},{5,3},{7,5},{8,14},{10,8},{12,... | collective-permute-start | bytes 1572872 | tf_op jit(solution)/shard_map/ppermute | solution.py:18
  152.7 31.6 %collective-permute-start.4 = (bf16[1024,256]{1,0:T(8,128)(2,1)}, bf16[1024,256]{1,0:T(8,128)(2,1)}, u32[]{:S(2)}, u32[]{:S(2)}) collective-permute-start(bf16[1024,256]{1,0:T(8,128)(2,1)} %collective-permute-done.3.refs_4_), channel_id=1, source_target_pairs={{0,2},{2,4},{4,6},{6,0},{1,3},{3,5},{5,7},{7,1},{8,10},{10,12},{12... | collective-permute-start | bytes 1572872 | tf_op jit(solution)/shard_map/ppermute | solution.py:18
  163.2 21.1 %collective-permute-start.9 = (bf16[1024,256]{1,0:T(8,128)(2,1)}, bf16[1024,256]{1,0:T(8,128)(2,1)}, u32[]{:S(2)}, u32[]{:S(2)}) collective-permute-start(bf16[1024,256]{1,0:T(8,128)(2,1)} %collective-permute-done.8.refs_11_), channel_id=1, source_target_pairs={{0,6},{2,0},{4,2},{6,4},{1,7},{3,1},{5,3},{7,5},{8,14},{10,8},{12,... | collective-permute-start | bytes 1572872 | tf_op jit(solution)/shard_map/ppermute | solution.py:18
